TPU v7x, 32 devices: a whole 2x2x4 slice. The times are simulated.
32 devices in a mesh: grp: 2 (over y), blk: 8 (over z, x), uly: 2 (over core).
Axes of the slice: x: 2, y: 2, z: 4, core: 2. Of those that a mesh axis runs over, the one named last changes fastest.
Arguments:
- query: bfloat16 [512, 1152], P(('grp', 'blk', 'uly')), parts along dimension 0, may hold values from -6 to 6
- key: bfloat16 [512, 1152], P(('grp', 'blk', 'uly')), parts along dimension 0, may hold values from -6 to 6
- value: bfloat16 [512, 1152], P(('grp', 'blk', 'uly')), parts along dimension 0, may hold values from -6 to 6
- q_gain: float32 [96], replicated, may hold values from 1 to 2.5
- k_gain: float32 [96], replicated, may hold values from 1 to 2.5
- out_weight: bfloat16 [1152, 2304], P('uly'), may hold values from -0.1875 to 0.1875
Outputs:
- mixed: bfloat16 [512, 2304], P(('grp', 'blk', 'uly')), parts along dimension 0
There are 2 independent parts, one for each index of `grp`. A program takes and returns all parts, laid end to end along the dimension named above; an argument that names none is the same for every part. Nothing has to cross between parts.
All inputs are finite; a program needn't handle non-finite values.
Results may differ from a plain program's by a relative error of at most 0.012.
Values may be sent and summed in bfloat16 or wider, within the bound.
A program may use at most 128 MiB of HBM per device.

v0:
```python
import jax
import jax.numpy as jnp
from jax import lax
from jax.sharding import PartitionSpec as P

H = 12
HD = 96


def partner_2(block, axis, apart):
    count = lax.axis_size(axis)
    route = []
    for low in range(count):
        high = low | 1 << apart
        if high != low and high < count:
            route += [(low, high), (high, low)]
    return lax.ppermute(block, axis, route)


def from_behind(value, axis, steps):
    count = lax.axis_size(axis)
    pairs = [(source, (source + steps) % count) for source in range(count)]
    return lax.ppermute(value, axis, pairs)


def normed(data, gain):
    tok_rows = data.shape[0]
    grid = data.astype(jnp.float32).reshape(tok_rows, H, HD)
    meansq = jnp.mean(grid * grid, axis=-1, keepdims=True)
    return (grid * lax.rsqrt(meansq + 1e-06) * gain).astype(jnp.bfloat16).reshape(tok_rows, H * HD)


def attend_block(query_heads, carry, kv_piece):
    weighted, total_weight = carry
    length = kv_piece.shape[1]
    head_count = query_heads.shape[1]
    key_heads = kv_piece[0].reshape(length, head_count, HD)
    value_heads = kv_piece[1].reshape(length, head_count, HD)
    score_scale = float(HD) ** (-0.5)
    scores = (
        jnp.einsum("qhd,khd->hqk", query_heads, key_heads, preferred_element_type=jnp.float32)
        * score_scale
    )
    expd = jnp.exp(scores)
    total_weight = total_weight + jnp.sum(expd, axis=-1).T
    weighted = weighted + jnp.einsum(
        "hqk,khd->qhd", expd.astype(jnp.bfloat16), value_heads, preferred_element_type=jnp.float32
    )
    return (weighted, total_weight)


def on_device(query, key, value, q_gain, k_gain, out_weight):
    query_normed = normed(query, q_gain)
    key_normed = normed(key, k_gain)
    query_group, key_group, value_group = (
        lax.all_to_all(query_normed, "uly", split_axis=1, concat_axis=0, tiled=True),
        lax.all_to_all(key_normed, "uly", split_axis=1, concat_axis=0, tiled=True),
        lax.all_to_all(value, "uly", split_axis=1, concat_axis=0, tiled=True),
    )
    row_count = query_group.shape[0]
    local_heads = query_group.shape[1] // HD
    half_heads = local_heads // 2
    half_width = half_heads * HD
    parity = lax.axis_index("blk") % 2
    stacked = jnp.stack([query_group, key_group, value_group])
    mine = lax.dynamic_slice_in_dim(stacked, parity * half_width, half_width, 2)
    others = lax.dynamic_slice_in_dim(stacked, (1 - parity) * half_width, half_width, 2)
    partner = partner_2(others, "blk", 0)
    paired = jnp.where(
        parity == 0, jnp.concatenate([mine, partner], 1), jnp.concatenate([partner, mine], 1)
    )
    pair_rows = 2 * row_count
    query_heads = paired[0].reshape(pair_rows, half_heads, HD)
    gathered = paired[1:3]
    members = lax.axis_size("blk") // 2
    held = 1
    while held < members:
        take = min(held, members - held)
        arrived = from_behind(gathered, "blk", 2 * held)
        gathered = jnp.concatenate([gathered, arrived], 1)
        held = held + take
    group_size = 1
    for factor in range(1, members + 1):
        if members % factor == 0 and factor * pair_rows <= 1024:
            group_size = factor
    block_rows = group_size * pair_rows
    block_count = members // group_size
    blocks = jnp.transpose(gathered.reshape(2, block_count, block_rows, half_width), (1, 0, 2, 3))

    def scan_step(carry, kv_piece):
        return (attend_block(query_heads, carry, kv_piece), None)

    start_carry = (
        jnp.zeros((pair_rows, half_heads, HD), jnp.float32),
        jnp.zeros((pair_rows, half_heads), jnp.float32),
    )
    (weighted, total_weight), unused = lax.scan(scan_step, start_carry, blocks)
    attn_pair = (
        (weighted / total_weight[:, :, None]).astype(jnp.bfloat16).reshape(pair_rows, half_width)
    )
    own_rows = lax.dynamic_slice_in_dim(attn_pair, parity * row_count, row_count, 0)
    send_rows = lax.dynamic_slice_in_dim(attn_pair, (1 - parity) * row_count, row_count, 0)
    returned = partner_2(send_rows, "blk", 0)
    attn = jnp.where(
        parity == 0,
        jnp.concatenate([own_rows, returned], 1),
        jnp.concatenate([returned, own_rows], 1),
    )
    attn_tokens = lax.all_to_all(attn, "uly", split_axis=0, concat_axis=1, tiled=True)
    mixed = jnp.dot(
        attn_tokens,
        lax.all_gather(out_weight, "uly", axis=0, tiled=True),
        preferred_element_type=jnp.float32,
    )
    return mixed.astype(jnp.bfloat16)


def solution(mesh):
    in_specs = (
        P(("grp", "blk", "uly"), None),
        P(("grp", "blk", "uly"), None),
        P(("grp", "blk", "uly"), None),
        P(),
        P(),
        P("uly", None),
    )
    out_specs = P(("grp", "blk", "uly"), None)
    return jax.shard_map(
        on_device, mesh=mesh, in_specs=in_specs, out_specs=out_specs, check_vma=False
    )
```

profile of v0, /device:TPU:0, one launch (start us, length us, event | category | flops | bytes accessed | tf_op | source)
XLA Modules:
  0.0 66.7 jit_solution(3177109753742246567)
XLA Ops:
  6.5 0.0 all-gather.2.cloned.1.call-start
  6.5 0.7 %all-gather.2.cloned.1.call-update = ((bf16[576,2304]{1,0:T(8,128)(2,1)}), bf16[1152,2304]{1,0:T(8,128)(2,1)}) async-update(((), (), s32[]{:S(2)}) %all-gather.2.cloned.1.call-start, bf16[576,2304]{1,0:T(8,128)(2,1)} %param.11) | async-update | bytes 10616856
  7.3 0.8 %convert_multiply_fusion.3 = f32[16,1152]{1,0:T(8,128)S(1)} fusion(bf16[16,1152]{1,0:T(8,128)(2,1)} %param.6), kind=kLoop, calls=%fused_computation.14 | loop fusion | flops 36864 | bytes 110592 | tf_op jit(solution)/shard_map/mul | solution.py:29
  8.0 0.1 mul.77
  8.1 0.1 reduce_sum.28
  8.3 0.1 mul.78
  8.4 0.1 mul.79
  8.5 0.7 mul.81
  9.1 0.1 mul.82
  9.2 0.8 %fusion.5 = bf16[16,1152]{1,0:T(8,128)(2,1)S(1)} fusion(f32[16,1152]{1,0:T(8,128)S(1)} %mul.79, bf16[16,1152]{1,0:T(8,128)(2,1)} %param.6, f32[1152]{0:T(1024)S(1)} %mul.82), kind=kLoop, calls=%fused_computation.16 | loop fusion | flops 73728 | bytes 152064 | tf_op jit(solution)/shard_map/convert_element_type | solution.py:30
  10.0 0.1 all_to_all.48
  10.1 0.6 copy.26
  10.7 3.3 %all-to-all-start = ((bf16[16,2,576]{2,0,1:T(8,128)(2,1)}), bf16[16,2,576]{2,0,1:T(8,128)(2,1)S(1)}, u32[]{:S(2)}, u32[]{:S(2)}) async-start(bf16[16,2,576]{2,0,1:T(8,128)(2,1)} %copy.26), calls=%async_computation | async-start | bytes 81920 | tf_op jit(solution)/shard_map/all_to_all | solution.py:56
  14.0 0.8 %convert_multiply_fusion.1 = f32[16,1152]{1,0:T(8,128)S(1)} fusion(bf16[16,1152]{1,0:T(8,128)(2,1)} %param.7), kind=kLoop, calls=%fused_computation.12 | loop fusion | flops 36864 | bytes 110592 | tf_op jit(solution)/shard_map/mul | solution.py:29
  14.8 0.1 mul.86
  14.9 0.1 reduce_sum.29
  15.0 0.1 mul.87
  15.1 0.1 mul.88
  15.2 0.7 mul.90
  15.9 0.1 mul.91
  16.0 0.8 %fusion.7 = bf16[16,1152]{1,0:T(8,128)(2,1)S(1)} fusion(f32[16,1152]{1,0:T(8,128)S(1)} %mul.88, bf16[16,1152]{1,0:T(8,128)(2,1)} %param.7, f32[1152]{0:T(1024)S(1)} %mul.91), kind=kLoop, calls=%fused_computation.18 | loop fusion | flops 73728 | bytes 152064 | tf_op jit(solution)/shard_map/convert_element_type | solution.py:30
  16.8 0.1 all_to_all.51
  16.9 0.9 %all_to_all.54 = bf16[16,2,576]{2,1,0:T(2,128)(2,1)S(1)} reshape(bf16[16,1152]{1,0:T(8,128)(2,1)} %param.8) | data formatting | bytes 73728 | tf_op jit(solution)/shard_map/all_to_all | solution.py:58
  17.8 0.0 all-to-all-done
  17.8 3.8 %all_to_all.64 = bf16[16,2,576]{2,0,1:T(8,128)(2,1)S(1)} all-to-all(bf16[16,2,576]{2,0,1:T(8,128)(2,1)S(1)} %copy.27), channel_id=1, replica_groups=mesh['grp'=2,'blk'=8,'uly'=2] {'uly'}, dimensions={1} | all-to-all | bytes 73728 | tf_op jit(solution)/shard_map/all_to_all | solution.py:57
  21.6 3.8 %all_to_all.65 = bf16[16,2,576]{2,0,1:T(8,128)(2,1)S(1)} all-to-all(bf16[16,2,576]{2,0,1:T(8,128)(2,1)S(1)} %copy.28), channel_id=1, replica_groups=mesh['grp'=2,'blk'=8,'uly'=2] {'uly'}, dimensions={1} | all-to-all | bytes 73728 | tf_op jit(solution)/shard_map/all_to_all | solution.py:58
  25.4 0.1 constant_dynamic-slice_fusion.3
  25.5 3.0 %collective-permute-start = (bf16[3,32,288]{2,1,0:T(8,128)(2,1)S(1)}, bf16[3,32,288]{2,1,0:T(8,128)(2,1)S(1)}, u32[]{:S(2)}, u32[]{:S(2)}) collective-permute-start(bf16[3,32,288]{2,1,0:T(8,128)(2,1)S(1)} %get-tuple-element.22), channel_id=1, source_target_pairs={{0,2},{2,0},{4,6},{6,4},{8,10},{10,8},{12,14},{14,12},{1,3},{3,1},... | collective-permute-start | bytes 165896 | tf_op jit(solution)/shard_map/ppermute | solution.py:17
  28.6 2.6 %collective-permute-done = bf16[3,32,288]{2,1,0:T(8,128)(2,1)S(1)} collective-permute-done((bf16[3,32,288]{2,1,0:T(8,128)(2,1)S(1)}, bf16[3,32,288]{2,1,0:T(8,128)(2,1)S(1)}, u32[]{:S(2)}, u32[]{:S(2)}) %collective-permute-start) | collective-permute-done | bytes 55328 | tf_op jit(solution)/shard_map/ppermute | solution.py:17
  31.2 1.9 %collective-permute-start.1 = (bf16[2,64,288]{2,1,0:T(8,128)(2,1)S(1)}, bf16[2,64,288]{2,1,0:T(8,128)(2,1)S(1)}, u32[]{:S(2)}, u32[]{:S(2)}) collective-permute-start(bf16[2,64,288]{2,1,0:T(8,128)(2,1)S(1)} %slice.19), channel_id=1, source_target_pairs={{0,4},{2,6},{4,8},{6,10},{8,12},{10,14},{12,0},{14,2},{1,5},{3,7},... | collective-permute-start | bytes 221192 | tf_op jit(solution)/shard_map/ppermute | solution.py:23
  33.1 4.6 %collective-permute-done.1 = bf16[2,64,288]{2,1,0:T(8,128)(2,1)S(1)} collective-permute-done((bf16[2,64,288]{2,1,0:T(8,128)(2,1)S(1)}, bf16[2,64,288]{2,1,0:T(8,128)(2,1)S(1)}, u32[]{:S(2)}, u32[]{:S(2)}) %collective-permute-start.1) | collective-permute-done | bytes 73760 | tf_op jit(solution)/shard_map/ppermute | solution.py:23
  37.7 1.1 %collective-permute-start.2 = (bf16[2,128,288]{2,1,0:T(8,128)(2,1)S(1)}, bf16[2,128,288]{2,1,0:T(8,128)(2,1)S(1)}, u32[]{:S(2)}, u32[]{:S(2)}) collective-permute-start(bf16[2,128,288]{2,1,0:T(8,128)(2,1)S(1)} %pad_maximum_fusion.1), channel_id=1, source_target_pairs={{0,8},{2,10},{4,12},{6,14},{8,0},{10,2},{12,4},{14,6},{1,9},{3,11}... | collective-permute-start | bytes 442376 | tf_op jit(solution)/shard_map/ppermute | solution.py:23
  38.8 0.1 reshape_squeeze.3
  38.9 8.1 %collective-permute-done.2 = bf16[2,128,288]{2,1,0:T(8,128)(2,1)S(1)} collective-permute-done((bf16[2,128,288]{2,1,0:T(8,128)(2,1)S(1)}, bf16[2,128,288]{2,1,0:T(8,128)(2,1)S(1)}, u32[]{:S(2)}, u32[]{:S(2)}) %collective-permute-start.2) | collective-permute-done | bytes 147488 | tf_op jit(solution)/shard_map/ppermute | solution.py:23
  47.1 0.1 copy.30
  47.2 0.1 copy.29
  47.4 0.3 fusion.10
  47.6 0.2 fusion.2
  47.9 0.1 reshape.55
  48.0 1.6 %collective-permute-start.3 = (bf16[32,288]{1,0:T(8,128)(2,1)S(1)}, bf16[32,288]{1,0:T(8,128)(2,1)S(1)}, u32[]{:S(2)}, u32[]{:S(2)}) collective-permute-start(bf16[32,288]{1,0:T(8,128)(2,1)S(1)} %get-tuple-element.25), channel_id=1, source_target_pairs={{0,2},{2,0},{4,6},{6,4},{8,10},{10,8},{12,14},{14,12},{1,3},{3,1},... | collective-permute-start | bytes 55304 | tf_op jit(solution)/shard_map/ppermute | solution.py:17
  49.5 2.3 %collective-permute-done.3 = bf16[32,288]{1,0:T(8,128)(2,1)S(1)} collective-permute-done((bf16[32,288]{1,0:T(8,128)(2,1)S(1)}, bf16[32,288]{1,0:T(8,128)(2,1)S(1)}, u32[]{:S(2)}, u32[]{:S(2)}) %collective-permute-start.3) | collective-permute-done | bytes 18464 | tf_op jit(solution)/shard_map/ppermute | solution.py:17
  51.9 0.1 maximum_select_fusion.1
  52.0 3.8 %all_to_all.66 = bf16[2,16,576]{2,1,0:T(8,128)(2,1)S(1)} all-to-all(bf16[2,16,576]{2,1,0:T(8,128)(2,1)S(1)} %maximum_select_fusion.1), channel_id=1, replica_groups=mesh['grp'=2,'blk'=8,'uly'=2] {'uly'}, dimensions={0} | all-to-all | bytes 73728 | tf_op jit(solution)/shard_map/all_to_all | solution.py:109
  55.8 0.1 all_to_all.59
  55.9 0.0 all-gather.2.cloned.1.call-done
  55.9 4.0 %convolution_convert_fusion = bf16[16,2304]{1,0:T(8,128)(2,1)} fusion(bf16[16,1152]{1,0:T(8,128)(2,1)S(1)} %all_to_all.59, bf16[1152,2304]{1,0:T(8,128)(2,1)} %all-gather.2.cloned.1.call-done), kind=kOutput, calls=%fused_computation | convolution fusion | flops 84971520 | bytes 5419008 | tf_op jit(solution)/shard_map/dot_general | solution.py:110
  (14 shorter events, 0.3 us)
Async XLA Ops:
  6.5 49.4 %all-gather.2.cloned.1.call-start = ((), (), s32[]{:S(2)}) async-start(), calls=%async_computation.4 | async-start | bytes 7962624 | tf_op jit(solution)/shard_map/all_gather | solution.py:112
  10.7 7.1 %all-to-all-start = ((bf16[16,2,576]{2,0,1:T(8,128)(2,1)}), bf16[16,2,576]{2,0,1:T(8,128)(2,1)S(1)}, u32[]{:S(2)}, u32[]{:S(2)}) async-start(bf16[16,2,576]{2,0,1:T(8,128)(2,1)} %copy.26), calls=%async_computation | async-start | bytes 81920 | tf_op jit(solution)/shard_map/all_to_all | solution.py:56
  25.5 5.6 %collective-permute-start = (bf16[3,32,288]{2,1,0:T(8,128)(2,1)S(1)}, bf16[3,32,288]{2,1,0:T(8,128)(2,1)S(1)}, u32[]{:S(2)}, u32[]{:S(2)}) collective-permute-start(bf16[3,32,288]{2,1,0:T(8,128)(2,1)S(1)} %get-tuple-element.22), channel_id=1, source_target_pairs={{0,2},{2,0},{4,6},{6,4},{8,10},{10,8},{12,14},{14,12},{1,3},{3,1},... | collective-permute-start | bytes 165896 | tf_op jit(solution)/shard_map/ppermute | solution.py:17
  31.2 6.5 %collective-permute-start.1 = (bf16[2,64,288]{2,1,0:T(8,128)(2,1)S(1)}, bf16[2,64,288]{2,1,0:T(8,128)(2,1)S(1)}, u32[]{:S(2)}, u32[]{:S(2)}) collective-permute-start(bf16[2,64,288]{2,1,0:T(8,128)(2,1)S(1)} %slice.19), channel_id=1, source_target_pairs={{0,4},{2,6},{4,8},{6,10},{8,12},{10,14},{12,0},{14,2},{1,5},{3,7},... | collective-permute-start | bytes 221192 | tf_op jit(solution)/shard_map/ppermute | solution.py:23
  37.7 9.3 %collective-permute-start.2 = (bf16[2,128,288]{2,1,0:T(8,128)(2,1)S(1)}, bf16[2,128,288]{2,1,0:T(8,128)(2,1)S(1)}, u32[]{:S(2)}, u32[]{:S(2)}) collective-permute-start(bf16[2,128,288]{2,1,0:T(8,128)(2,1)S(1)} %pad_maximum_fusion.1), channel_id=1, source_target_pairs={{0,8},{2,10},{4,12},{6,14},{8,0},{10,2},{12,4},{14,6},{1,9},{3,11}... | collective-permute-start | bytes 442376 | tf_op jit(solution)/shard_map/ppermute | solution.py:23
  48.0 3.9 %collective-permute-start.3 = (bf16[32,288]{1,0:T(8,128)(2,1)S(1)}, bf16[32,288]{1,0:T(8,128)(2,1)S(1)}, u32[]{:S(2)}, u32[]{:S(2)}) collective-permute-start(bf16[32,288]{1,0:T(8,128)(2,1)S(1)} %get-tuple-element.25), channel_id=1, source_target_pairs={{0,2},{2,0},{4,6},{6,4},{8,10},{10,8},{12,14},{14,12},{1,3},{3,1},... | collective-permute-start | bytes 55304 | tf_op jit(solution)/shard_map/ppermute | solution.py:17
Sparse Core Ops, SparseCore 0:
  8.9 18.0 all-gather.1
where the time goes:
time: 67.4 us; the launch traced here: 66.7 us
  waiting for transfers between devices  18.3 us (27%)
  between operations  13.6 us (20%)
  blocking collectives  11.3 us (17%)
  starting transfers between devices  10.9 us (16%)
  local copies, waits for them, and re-layouts  4.6 us (7%)
  matrix products  4.39 us (7%)
  other arithmetic  3.56 us (5%)
    ppermute x2, waiting for transfers between devices, from_behind(): return lax.ppermute(value, axis, pairs)  12.7 us
    ppermute x2, waiting for transfers between devices, partner_2(): return lax.ppermute(block, axis, route)  4.91 us
    ppermute x2, starting transfers between devices, partner_2(): return lax.ppermute(block, axis, route)  4.59 us
    dot_general x1, matrix products, on_device(): jnp.dot(attn_tokens, lax.all_gather(out_weight, 'uly', axis=0, tiled=True...  3.96 us
    all_to_all x1, blocking collectives, on_device(): lax.all_to_all(value, 'uly', split_axis=1, concat_axis=0, tiled=True)  3.78 us
    all_to_all x1, blocking collectives, on_device(): lax.all_to_all(attn, 'uly', split_axis=0, concat_axis=1, tiled=True)  3.76 us
    all_to_all x1, blocking collectives, on_device(): lax.all_to_all(key_normed, 'uly', split_axis=1, concat_axis=0, tiled=True)  3.76 us
    all_to_all x1, starting transfers between devices, on_device(): lax.all_to_all(query_normed, 'uly', split_axis=1, concat_axis=0, tiled=True)  3.27 us
  transfers between devices with their start and end apart: 6, of which 4 were waited for; matrix products, arithmetic and copies ran while one was open for 11% of the time, Pallas kernels for 0%

commit v1 on v0

v1 whole, which is shorter than its diff:
```python
import functools

import jax
import jax.numpy as jnp
from jax import lax
from jax.experimental import pallas as pl
from jax.experimental.pallas import tpu as pltpu
from jax.sharding import PartitionSpec as P

HD = 96
LANES = 128
MESH = pl.DeviceIdType.MESH


def loop(count, body):
    if count <= 32:
        for i in range(count):
            body(i)
    else:
        lax.fori_loop(0, count, lambda i, c: (body(i), c)[1], 0)


def layer_kernel(
    blks, ulys, heads, copies,
    q_hbm, k_hbm, v_hbm, qg_ref, kg_ref, w_hbm, out_ref,
    raw, w_vmem, pack, qkv, attn, back, mine, away, arrived,
    load_sem, w_sem, send1, recv1, send2, recv2, send3, recv3,
):
    n = blks * ulys
    rows = raw.shape[1]
    owners = heads * copies
    blk, uly = lax.axis_index("blk"), lax.axis_index("uly")
    me = blk * ulys + uly
    chip_rows = rows * ulys
    core_heads = heads // ulys
    seq = n * rows
    block = seq // copies
    chips = block // chip_rows

    loads = [
        pltpu.make_async_copy(src, raw.at[i], load_sem.at[i])
        for i, src in enumerate((q_hbm, k_hbm, v_hbm))
    ]
    for one in loads:
        one.start()
    load_w = pltpu.make_async_copy(w_hbm, w_vmem, w_sem)
    load_w.start()

    def mirror(d):
        plane = d // 4
        return d + (plane % 2) * (3 - 2 * (d % 4))

    def owner_device(o):
        return mirror(o * n // owners)

    spot = mirror(me)
    slot = (spot * owners + n - 1) // n
    is_owner = jnp.logical_and(slot < owners, (slot * n) // owners == spot)
    slot = jnp.minimum(slot, owners - 1)

    barrier = pltpu.get_barrier_semaphore()

    def greet(i):
        d = lax.rem(me + 1 + i, n)
        pl.semaphore_signal(
            barrier, inc=1, device_id={"blk": d // ulys, "uly": d % ulys}, device_id_type=MESH
        )

    loop(n - 1, greet)

    pad = jnp.zeros((rows, LANES - HD), jnp.bfloat16)
    for i, gain_ref in ((0, qg_ref), (1, kg_ref)):
        loads[i].wait()
        gain = gain_ref[...]
        for h in range(heads):
            x = raw[i, :, h * HD:(h + 1) * HD].astype(jnp.float32)
            scale = lax.rsqrt(jnp.mean(x * x, axis=-1, keepdims=True) + 1e-06)
            normed = (x * scale * gain).astype(jnp.bfloat16)
            pack[h, :, i * LANES:(i + 1) * LANES] = jnp.concatenate([normed, pad], axis=1)
    loads[2].wait()
    for h in range(heads):
        x = raw[2, :, h * HD:(h + 1) * HD]
        pack[h, :, 2 * LANES:3 * LANES] = jnp.concatenate([x, pad], axis=1)

    pl.semaphore_wait(barrier, n - 1)

    my_rows = pl.ds(pl.multiple_of(me * rows, rows), rows)

    def send_of(o):
        d = owner_device(o)
        return d, pltpu.make_async_remote_copy(
            src_ref=pack.at[o // copies],
            dst_ref=qkv.at[my_rows],
            send_sem=send1.at[o],
            recv_sem=recv1.at[me],
            device_id={"blk": d // ulys, "uly": d % ulys},
            device_id_type=MESH,
        )

    start_at = (me * owners) // n + owners // 2

    def send(i):
        d, copy = send_of(lax.rem(start_at + i, owners))

        @pl.when(d != me)
        def _():
            copy.start()

    loop(owners, send)

    @pl.when(is_owner)
    def _():
        head = slot // copies
        part = slot % copies
        qkv[my_rows, :] = pack[head]

        def got(i):
            d = lax.rem(me + 1 + i, n)
            pltpu.make_async_remote_copy(
                src_ref=pack.at[0],
                dst_ref=qkv.at[pl.ds(pl.multiple_of(d * rows, rows), rows)],
                send_sem=send1.at[0],
                recv_sem=recv1.at[d],
                device_id={"blk": blk, "uly": uly},
                device_id_type=MESH,
            ).wait_recv()

        loop(n - 1, got)
        query = qkv[pl.ds(pl.multiple_of(part * block, block), block), 0:LANES]
        score_scale = float(HD) ** (-0.5)

        def step(j, carry):
            weighted, total = carry
            here = pl.ds(j * block, block)
            keys = qkv[here, LANES:2 * LANES]
            values = qkv[here, 2 * LANES:3 * LANES]
            scores = lax.dot_general(
                query, keys, (((1,), (1,)), ((), ())), preferred_element_type=jnp.float32
            ) * score_scale
            expd = jnp.exp(scores)
            total = total + jnp.sum(expd, axis=-1, keepdims=True)
            weighted = weighted + jnp.dot(
                expd.astype(jnp.bfloat16), values, preferred_element_type=jnp.float32
            )
            return weighted, total

        carry = (jnp.zeros((block, LANES), jnp.float32), jnp.zeros((block, 1), jnp.float32))
        if copies == 1:
            weighted, total = step(0, carry)
        else:
            weighted, total = lax.fori_loop(
                0, copies, lambda j, c: step(pl.multiple_of(j, 1), c), carry
            )
        attn[...] = (weighted / total).astype(jnp.bfloat16)

        to_core = head // core_heads
        place = head % core_heads

        def result_copy(i):
            chip = part * chips + i
            return chip, pltpu.make_async_remote_copy(
                src_ref=attn.at[pl.ds(i * chip_rows, chip_rows)],
                dst_ref=back.at[place],
                send_sem=send2.at[i],
                recv_sem=recv2.at[place],
                device_id={"blk": chip, "uly": to_core},
                device_id_type=MESH,
            )

        def local_copy(i):
            return pltpu.make_async_copy(
                attn.at[pl.ds(i * chip_rows, chip_rows)], back.at[place], recv2.at[place]
            )

        def give(i):
            chip, copy = result_copy(i)
            home = chip * ulys + to_core == me

            @pl.when(home)
            def _():
                local_copy(i).start()

            @pl.when(jnp.logical_not(home))
            def _():
                copy.start()

        loop(chips, give)

        def given(i):
            chip, copy = result_copy(i)

            @pl.when(chip * ulys + to_core != me)
            def _():
                copy.wait_send()

        loop(chips, given)

    for h in range(core_heads):
        pltpu.make_async_copy(attn.at[pl.ds(0, chip_rows)], back.at[h], recv2.at[h]).wait()

    own_rows = pl.ds(pl.multiple_of(uly * rows, rows), rows)
    other_rows = pl.ds(pl.multiple_of((1 - uly) * rows, rows), rows)
    lhs = jnp.concatenate(
        [
            jnp.concatenate([back[h, other_rows, 0:HD] for h in range(core_heads)], axis=1),
            jnp.concatenate([back[h, own_rows, 0:HD] for h in range(core_heads)], axis=1),
        ],
        axis=0,
    )
    load_w.wait()
    pieces = send3.shape[0]
    width = out_ref.shape[1] // pieces
    swaps = []
    for c in range(pieces):
        cols = slice(c * width, (c + 1) * width)
        part_out = jnp.dot(lhs, w_vmem[:, cols], preferred_element_type=jnp.float32)
        away[c] = part_out[:rows]
        mine[c] = part_out[rows:]
        swap = pltpu.make_async_remote_copy(
            src_ref=away.at[c],
            dst_ref=arrived.at[c],
            send_sem=send3.at[c],
            recv_sem=recv3.at[c],
            device_id={"blk": blk, "uly": 1 - uly},
            device_id_type=MESH,
        )
        swap.start()
        swaps.append(swap)
    for c in range(pieces):
        swaps[c].wait_recv()
        out_ref[:, c * width:(c + 1) * width] = (mine[c] + arrived[c]).astype(out_ref.dtype)

    for swap in swaps:
        swap.wait_send()

    def sent(o):
        d, copy = send_of(o)

        @pl.when(d != me)
        def _():
            copy.wait_send()

    loop(owners, sent)


def on_device(blks, ulys, query, key, value, q_gain, k_gain, out_weight):
    rows, width = query.shape
    heads = width // HD
    n = blks * ulys
    copies = 1
    while heads * copies * 2 <= n:
        copies *= 2
    owners = heads * copies
    depth, cols = out_weight.shape
    seq = n * rows
    block = seq // copies
    chip_rows = rows * ulys
    pieces = 3
    dma = pltpu.SemaphoreType.DMA
    return pl.pallas_call(
        functools.partial(layer_kernel, blks, ulys, heads, copies),
        out_shape=jax.ShapeDtypeStruct((rows, cols), jnp.bfloat16),
        in_specs=[
            pl.BlockSpec(memory_space=pl.ANY),
            pl.BlockSpec(memory_space=pl.ANY),
            pl.BlockSpec(memory_space=pl.ANY),
            pl.BlockSpec(memory_space=pltpu.VMEM),
            pl.BlockSpec(memory_space=pltpu.VMEM),
            pl.BlockSpec(memory_space=pl.ANY),
        ],
        out_specs=pl.BlockSpec(memory_space=pltpu.VMEM),
        scratch_shapes=[
            pltpu.VMEM((3, rows, width), jnp.bfloat16),
            pltpu.VMEM((depth, cols), jnp.bfloat16),
            pltpu.VMEM((heads, rows, 3 * LANES), jnp.bfloat16),
            pltpu.VMEM((seq, 3 * LANES), jnp.bfloat16),
            pltpu.VMEM((block, LANES), jnp.bfloat16),
            pltpu.VMEM((heads // ulys, chip_rows, LANES), jnp.bfloat16),
            pltpu.VMEM((pieces, rows, cols // pieces), jnp.float32),
            pltpu.VMEM((pieces, rows, cols // pieces), jnp.float32),
            pltpu.VMEM((pieces, rows, cols // pieces), jnp.float32),
            dma((3,)),
            dma,
            dma((owners,)),
            dma((n,)),
            dma((block // chip_rows,)),
            dma((heads // ulys,)),
            dma((pieces,)),
            dma((pieces,)),
        ],
        compiler_params=pltpu.CompilerParams(collective_id=0, has_side_effects=True),
    )(query, key, value, q_gain.reshape(1, HD), k_gain.reshape(1, HD), out_weight)


def solution(mesh):
    blks, ulys = mesh.shape["blk"], mesh.shape["uly"]
    tokens = P(("grp", "blk", "uly"), None)
    return jax.shard_map(
        functools.partial(on_device, blks, ulys),
        mesh=mesh,
        in_specs=(tokens, tokens, tokens, P(), P(), P("uly", None)),
        out_specs=tokens,
        check_vma=False,
    )
```

time: 67.4 us -> 20.5 us (0.30)
  Pallas kernels: 0 us -> 18.8 us
  waiting for transfers between devices: 18.3 us -> 0 us
  between operations: 13.6 us -> 0.01 us
  blocking collectives: 11.3 us -> 0 us
  starting transfers between devices: 10.9 us -> 0 us
  matrix products: 4.39 us -> 0 us
  other arithmetic: 3.56 us -> 0 us
  local copies, waits for them, and re-layouts: 4.6 us -> 1.52 us
    pallas_call x0 -> x1, Pallas kernels: none -> 18.8 us  [on_device(): pl.pallas_call(functools.partial(layer_kernel, blks, ulys, heads, copies)...]
    ppermute x4 -> x0, waiting for transfers between devices: 17.6 us -> none  [the longest x2 12.7 us: from_behind(): return lax.ppermute(value, axis, pairs)]
    all_to_all x3 -> x0, blocking collectives: 11.3 us -> none  [the longest x1 3.78 us: on_device(): lax.all_to_all(value, 'uly', split_axis=1, concat_axis=0, tiled=True)]
    ppermute x4 -> x0, starting transfers between devices: 7.62 us -> none  [the longest x2 4.59 us: partner_2(): return lax.ppermute(block, axis, route)]
    dot_general x3 -> x0, matrix products: 4.39 us -> none  [the longest x1 3.96 us: on_device(): jnp.dot(attn_tokens, lax.all_gather(out_weight, 'uly', axis=0, tiled=True...]
    all_to_all x1 -> x0, starting transfers between devices: 3.27 us -> none  [on_device(): lax.all_to_all(query_normed, 'uly', split_axis=1, concat_axis=0, tiled=True)]
    mul x10 -> x0, local copies, waits for them, and re-layouts: 2.05 us -> none  [the longest x8 1.84 us: normed(): grid * lax.rsqrt(meansq + 1e-06) * gain]
    all_to_all x8 -> x0, local copies, waits for them, and re-layouts: 1.88 us -> none  [the longest x2 0.89 us: on_device(): lax.all_to_all(value, 'uly', split_axis=1, concat_axis=0, tiled=True)]
  transfers between devices with their start and end apart: 6 -> 0, of which waited for: 4 -> 0; matrix products, arithmetic and copies ran while one was open for 11% -> 0% of each run, Pallas kernels for 0% -> 0%
where the time goes in v1:
time: 20.5 us; the launch traced here: 20.3 us
  Pallas kernels  18.8 us (92%)
  local copies, waits for them, and re-layouts  1.52 us (7%)
    pallas_call x1, Pallas kernels, on_device(): pl.pallas_call(functools.partial(layer_kernel, blks, ulys, heads, copies)...  18.8 us
    unnamed x1, local copies, waits for them, and re-layouts  1.52 us

profile of v1, /device:TPU:0, one launch (start us, length us, event | category | flops | bytes accessed | tf_op | source)
XLA Modules:
  0.0 20.3 jit_solution(12824470575719967226)
XLA Ops:
  0.0 18.8 %shard_map.64 = bf16[16,2304]{1,0:T(8,128)(2,1)} custom-call(bf16[16,1152]{1,0:T(8,128)(2,1)} %q_hbm.1, bf16[16,1152]{1,0:T(8,128)(2,1)} %k_hbm.1, bf16[16,1152]{1,0:T(8,128)(2,1)} %v_hbm.1, f32[1,96]{1,0:T(1,128)} %bitcast.2, f32[1,96]{1,0:T(1,128)} %bitcast.3, bf16[576,2304]{1,0:T(8,128)(2,1)} %w_hbm.1), custom_call_target="tpu_custom_call" | custom-call | tf_op jit(solution)/shard_map/pallas_call | solution.py:260
  18.8 1.5 %copy.8 = bf16[16,2304]{1,0:T(8,128)(2,1)} copy(bf16[16,2304]{1,0:T(8,128)(2,1)} %shard_map.64) | data formatting | bytes 147456

commit v2 on v1

v2 whole, which is shorter than its diff:
```python
import functools

import jax
import jax.numpy as jnp
from jax import lax
from jax.experimental import pallas as pl
from jax.experimental.pallas import tpu as pltpu
from jax.sharding import PartitionSpec as P

HD = 96
LANES = 128
CHUNKS = 4
MESH = pl.DeviceIdType.MESH


def loop(count, body):
    if count <= 32:
        for i in range(count):
            body(i)
    else:
        lax.fori_loop(0, count, lambda i, c: (body(i), c)[1], 0)


def layer_kernel(
    blks, ulys, heads, copies,
    q_hbm, k_hbm, v_hbm, qg_hbm, kg_hbm, w_hbm, out_ref,
    raw, gains, w_vmem, pack, qkv, attn, back, acc,
    load_sem, gain_sem, w_sem, send1, recv1, send2, recv2, send_w, recv_w,
):
    n = blks * ulys
    rows = raw.shape[1]
    owners = heads * copies
    blk, uly = lax.axis_index("blk"), lax.axis_index("uly")
    me = blk * ulys + uly
    seq = n * rows
    block = seq // copies
    chunk = attn.shape[1]
    chunks = attn.shape[0]
    targets = chunk // rows
    depth = w_hbm.shape[0]
    upper = (2 * me) // n

    loads = [
        pltpu.make_async_copy(src, raw.at[i], load_sem.at[i])
        for i, src in enumerate((q_hbm, k_hbm, v_hbm))
    ]
    load_gains = [
        pltpu.make_async_copy(src, gains.at[i], gain_sem.at[i])
        for i, src in enumerate((qg_hbm, kg_hbm))
    ]
    for one in loads + load_gains:
        one.start()

    def mirror(d):
        plane = d // 4
        return d + (plane % 2) * (3 - 2 * (d % 4))

    def owner_device(o):
        return mirror(o * n // owners)

    spot = mirror(me)
    slot = (spot * owners + n - 1) // n
    is_owner = jnp.logical_and(slot < owners, (slot * n) // owners == spot)
    slot = jnp.minimum(slot, owners - 1)

    barrier = pltpu.get_barrier_semaphore()

    def greet(i):
        d = lax.rem(me + 1 + i, n)
        pl.semaphore_signal(
            barrier, inc=1, device_id={"blk": d // ulys, "uly": d % ulys}, device_id_type=MESH
        )

    loop(n - 1, greet)

    my_depth = pl.ds(pl.multiple_of(uly * depth, depth), depth)
    load_w = pltpu.make_async_copy(w_hbm, w_vmem.at[my_depth], w_sem)
    load_w.start()

    pad = jnp.zeros((rows, LANES - HD), jnp.bfloat16)
    for i in range(2):
        loads[i].wait()
        load_gains[i].wait()
        gain = gains[i]
        for h in range(heads):
            x = raw[i, :, h * HD:(h + 1) * HD].astype(jnp.float32)
            scale = lax.rsqrt(jnp.mean(x * x, axis=-1, keepdims=True) + 1e-06)
            normed = (x * scale * gain).astype(jnp.bfloat16)
            pack[h, :, i * LANES:(i + 1) * LANES] = jnp.concatenate([normed, pad], axis=1)
    loads[2].wait()
    for h in range(heads):
        x = raw[2, :, h * HD:(h + 1) * HD]
        pack[h, :, 2 * LANES:3 * LANES] = jnp.concatenate([x, pad], axis=1)

    pl.semaphore_wait(barrier, n - 1)

    my_rows = pl.ds(pl.multiple_of(me * rows, rows), rows)

    def send_of(o):
        d = owner_device(o)
        return d, pltpu.make_async_remote_copy(
            src_ref=pack.at[o // copies],
            dst_ref=qkv.at[my_rows],
            send_sem=send1.at[o],
            recv_sem=recv1.at[me],
            device_id={"blk": d // ulys, "uly": d % ulys},
            device_id_type=MESH,
        )

    start_at = (me * owners) // n + owners // 2

    def send(i):
        d, copy = send_of(lax.rem(start_at + i, owners))

        @pl.when(d != me)
        def _():
            copy.start()

    loop(owners, send)

    give_w = pltpu.make_async_remote_copy(
        src_ref=w_hbm,
        dst_ref=w_vmem.at[my_depth],
        send_sem=send_w,
        recv_sem=recv_w,
        device_id={"blk": blk, "uly": 1 - uly},
        device_id_type=MESH,
    )
    give_w.start()

    @pl.when(is_owner)
    def _():
        head = slot // copies
        part = slot % copies
        qkv[my_rows, :] = pack[head]

        def got(i):
            d = lax.rem(me + 1 + i, n)
            pltpu.make_async_remote_copy(
                src_ref=pack.at[0],
                dst_ref=qkv.at[pl.ds(pl.multiple_of(d * rows, rows), rows)],
                send_sem=send1.at[0],
                recv_sem=recv1.at[d],
                device_id={"blk": blk, "uly": uly},
                device_id_type=MESH,
            ).wait_recv()

        loop(n - 1, got)
        score_scale = float(HD) ** (-0.5)

        def step(query, j, carry):
            weighted, total = carry
            here = pl.ds(j * block, block)
            keys = qkv[here, LANES:2 * LANES]
            values = qkv[here, 2 * LANES:3 * LANES]
            scores = lax.dot_general(
                query, keys, (((1,), (1,)), ((), ())), preferred_element_type=jnp.float32
            ) * score_scale
            expd = jnp.exp(scores)
            total = total + jnp.sum(expd, axis=-1, keepdims=True)
            weighted = weighted + jnp.dot(
                expd.astype(jnp.bfloat16), values, preferred_element_type=jnp.float32
            )
            return weighted, total

        def result_copies(c):
            for i in range(targets):
                d = (part * chunks + c) * targets + i
                src = attn.at[c, pl.ds(i * rows, rows)]
                yield (
                    d == me,
                    functools.partial(
                        pltpu.make_async_copy, src, back.at[head], recv2.at[head]
                    ),
                    pltpu.make_async_remote_copy(
                        src_ref=src,
                        dst_ref=back.at[head],
                        send_sem=send2.at[c * targets + i],
                        recv_sem=recv2.at[head],
                        device_id={"blk": d // ulys, "uly": d % ulys},
                        device_id_type=MESH,
                    ),
                )

        for k in range(chunks):
            c = chunks - 1 - k + upper * (2 * k + 1 - chunks)
            at = part * block + c * chunk
            query = qkv[pl.ds(pl.multiple_of(at, chunk), chunk), 0:LANES]
            carry = (jnp.zeros((chunk, LANES), jnp.float32), jnp.zeros((chunk, 1), jnp.float32))
            if copies == 1:
                weighted, total = step(query, 0, carry)
            else:
                weighted, total = lax.fori_loop(
                    0, copies, functools.partial(lambda q, j, c: step(q, j, c), query), carry
                )
            attn[c] = (weighted / total).astype(jnp.bfloat16)
            for home, local, remote in result_copies(c):
                pl.when(home)(lambda local=local: local().start())
                pl.when(jnp.logical_not(home))(remote.start)

        for c in range(chunks):
            for home, _, remote in result_copies(c):
                pl.when(jnp.logical_not(home))(remote.wait_send)

    load_w.wait()
    give_w.wait_recv()
    first = (me * heads) // n
    for i in range(heads):
        h = lax.rem(first + i * (1 - 2 * upper) + heads, heads)
        pltpu.make_async_copy(attn.at[0, pl.ds(0, rows)], back.at[h], recv2.at[h]).wait()
        term = jnp.dot(
            back[h, :, 0:HD],
            w_vmem[pl.ds(pl.multiple_of(h * HD, HD), HD), :],
            preferred_element_type=jnp.float32,
        )
        if i == 0:
            acc[...] = term
        elif i < heads - 1:
            acc[...] += term
        else:
            out_ref[...] = (acc[...] + term).astype(out_ref.dtype)

    give_w.wait_send()

    def sent(o):
        d, copy = send_of(o)

        @pl.when(d != me)
        def _():
            copy.wait_send()

    loop(owners, sent)


def on_device(blks, ulys, query, key, value, q_gain, k_gain, out_weight):
    rows, width = query.shape
    heads = width // HD
    n = blks * ulys
    copies = 1
    while heads * copies * 2 <= n:
        copies *= 2
    owners = heads * copies
    depth, cols = out_weight.shape
    seq = n * rows
    block = seq // copies
    chunks = CHUNKS
    dma = pltpu.SemaphoreType.DMA
    return pl.pallas_call(
        functools.partial(layer_kernel, blks, ulys, heads, copies),
        out_shape=pltpu.VMEM((rows, cols), jnp.bfloat16),
        in_specs=[pl.BlockSpec(memory_space=pltpu.HBM)] * 6,
        out_specs=pl.BlockSpec(memory_space=pltpu.VMEM),
        scratch_shapes=[
            pltpu.VMEM((3, rows, width), jnp.bfloat16),
            pltpu.VMEM((2, 1, HD), jnp.float32),
            pltpu.VMEM((width, cols), jnp.bfloat16),
            pltpu.VMEM((heads, rows, 3 * LANES), jnp.bfloat16),
            pltpu.VMEM((seq, 3 * LANES), jnp.bfloat16),
            pltpu.VMEM((chunks, block // chunks, LANES), jnp.bfloat16),
            pltpu.VMEM((heads, rows, LANES), jnp.bfloat16),
            pltpu.VMEM((rows, cols), jnp.float32),
            dma((3,)),
            dma((2,)),
            dma,
            dma((owners,)),
            dma((n,)),
            dma((block // rows,)),
            dma((heads,)),
            dma,
            dma,
        ],
        compiler_params=pltpu.CompilerParams(collective_id=0, has_side_effects=True),
    )(query, key, value, q_gain.reshape(1, HD), k_gain.reshape(1, HD), out_weight)


def solution(mesh):
    blks, ulys = mesh.shape["blk"], mesh.shape["uly"]
    tokens = P(("grp", "blk", "uly"), None)
    return jax.shard_map(
        functools.partial(on_device, blks, ulys),
        mesh=mesh,
        in_specs=(tokens, tokens, tokens, P(), P(), P("uly", None)),
        out_specs=tokens,
        check_vma=False,
    )
```

time: 20.5 us -> 17.2 us (0.84)
  Pallas kernels: 18.8 us -> 16.5 us
  local copies, waits for them, and re-layouts: 1.52 us -> 0.64 us
    pallas_call x1, Pallas kernels: 18.8 us -> 16.5 us  [on_device(): pl.pallas_call(functools.partial(layer_kernel, blks, ulys, heads, copies)...]
    unnamed x1, local copies, waits for them, and re-layouts: 1.52 us -> 0.64 us
where the time goes in v2:
time: 17.2 us; the launch traced here: 17.1 us
  Pallas kernels  16.5 us (96%)
  local copies, waits for them, and re-layouts  0.64 us (4%)
    pallas_call x1, Pallas kernels, on_device(): pl.pallas_call(functools.partial(layer_kernel, blks, ulys, heads, copies)...  16.5 us
    unnamed x1, local copies, waits for them, and re-layouts  0.64 us

profile of v2, /device:TPU:0, one launch (start us, length us, event | category | flops | bytes accessed | tf_op | source)
XLA Modules:
  0.0 17.1 jit_solution(2807211935712302794)
XLA Ops:
  0.0 16.5 %shard_map.64 = bf16[16,2304]{1,0:T(8,128)(2,1)S(1)} custom-call(bf16[16,1152]{1,0:T(8,128)(2,1)} %q_hbm.1, bf16[16,1152]{1,0:T(8,128)(2,1)} %k_hbm.1, bf16[16,1152]{1,0:T(8,128)(2,1)} %v_hbm.1, f32[1,96]{1,0:T(1,128)} %bitcast.2, f32[1,96]{1,0:T(1,128)} %bitcast.3, bf16[576,2304]{1,0:T(8,128)(2,1)} %w_hbm.1), custom_call_target="tpu_custom_call" | custom-call | tf_op jit(solution)/shard_map/pallas_call | solution.py:248
  16.5 0.6 %copy.8 = bf16[16,2304]{1,0:T(8,128)(2,1)} copy(bf16[16,2304]{1,0:T(8,128)(2,1)S(1)} %shard_map.64) | data formatting | bytes 147456

commit v3 on v2

--- a/solution.py
+++ b/solution.py
@@ -9,7 +9,8 @@
 
 HD = 96
 LANES = 128
-CHUNKS = 4
+CHUNKS = 1
+GROUPS = 4
 MESH = pl.DeviceIdType.MESH
 
 
@@ -19,6 +20,10 @@
             body(i)
     else:
         lax.fori_loop(0, count, lambda i, c: (body(i), c)[1], 0)
+
+
+def take(ref, sem):
+    pltpu.make_async_copy(ref, ref, sem).wait()
 
 
 def layer_kernel(
@@ -34,18 +39,30 @@
     me = blk * ulys + uly
     seq = n * rows
     block = seq // copies
-    chunk = attn.shape[1]
-    chunks = attn.shape[0]
+    chunks = CHUNKS
+    chunk = block // chunks
+    groups = recv2.shape[0]
+    members = heads // groups
     targets = chunk // rows
     depth = w_hbm.shape[0]
     upper = (2 * me) // n
+
+    barrier = pltpu.get_barrier_semaphore()
+
+    def greet(i):
+        d = lax.rem(me + n // 2 + i + i // (n // 2), n)
+        pl.semaphore_signal(
+            barrier, inc=1, device_id={"blk": d // ulys, "uly": d % ulys}, device_id_type=MESH
+        )
+
+    loop(n - 1, greet)
 
     loads = [
         pltpu.make_async_copy(src, raw.at[i], load_sem.at[i])
         for i, src in enumerate((q_hbm, k_hbm, v_hbm))
     ]
     load_gains = [
-        pltpu.make_async_copy(src, gains.at[i], gain_sem.at[i])
+        pltpu.make_async_copy(src, gains.at[i], gain_sem)
         for i, src in enumerate((qg_hbm, kg_hbm))
     ]
     for one in loads + load_gains:
@@ -63,24 +80,14 @@
     is_owner = jnp.logical_and(slot < owners, (slot * n) // owners == spot)
     slot = jnp.minimum(slot, owners - 1)
 
-    barrier = pltpu.get_barrier_semaphore()
-
-    def greet(i):
-        d = lax.rem(me + 1 + i, n)
-        pl.semaphore_signal(
-            barrier, inc=1, device_id={"blk": d // ulys, "uly": d % ulys}, device_id_type=MESH
-        )
-
-    loop(n - 1, greet)
-
     my_depth = pl.ds(pl.multiple_of(uly * depth, depth), depth)
     load_w = pltpu.make_async_copy(w_hbm, w_vmem.at[my_depth], w_sem)
     load_w.start()
 
     pad = jnp.zeros((rows, LANES - HD), jnp.bfloat16)
+    take(gains, gain_sem)
     for i in range(2):
         loads[i].wait()
-        load_gains[i].wait()
         gain = gains[i]
         for h in range(heads):
             x = raw[i, :, h * HD:(h + 1) * HD].astype(jnp.float32)
@@ -101,16 +108,14 @@
         return d, pltpu.make_async_remote_copy(
             src_ref=pack.at[o // copies],
             dst_ref=qkv.at[my_rows],
-            send_sem=send1.at[o],
-            recv_sem=recv1.at[me],
+            send_sem=send1,
+            recv_sem=recv1,
             device_id={"blk": d // ulys, "uly": d % ulys},
             device_id_type=MESH,
         )
 
-    start_at = (me * owners) // n + owners // 2
-
     def send(i):
-        d, copy = send_of(lax.rem(start_at + i, owners))
+        d, copy = send_of(owners - 1 - i + upper * (2 * i + 1 - owners))
 
         @pl.when(d != me)
         def _():
@@ -134,18 +139,7 @@
         part = slot % copies
         qkv[my_rows, :] = pack[head]
 
-        def got(i):
-            d = lax.rem(me + 1 + i, n)
-            pltpu.make_async_remote_copy(
-                src_ref=pack.at[0],
-                dst_ref=qkv.at[pl.ds(pl.multiple_of(d * rows, rows), rows)],
-                send_sem=send1.at[0],
-                recv_sem=recv1.at[d],
-                device_id={"blk": blk, "uly": uly},
-                device_id_type=MESH,
-            ).wait_recv()
-
-        loop(n - 1, got)
+        take(qkv.at[pl.ds(0, (n - 1) * rows)], recv1)
         score_scale = float(HD) ** (-0.5)
 
         def step(query, j, carry):
@@ -166,17 +160,17 @@
         def result_copies(c):
             for i in range(targets):
                 d = (part * chunks + c) * targets + i
-                src = attn.at[c, pl.ds(i * rows, rows)]
+                src = attn.at[pl.ds(pl.multiple_of((c * targets + i) * rows, rows), rows)]
                 yield (
                     d == me,
                     functools.partial(
-                        pltpu.make_async_copy, src, back.at[head], recv2.at[head]
+                        pltpu.make_async_copy, src, back.at[head], recv2.at[head // members]
                     ),
                     pltpu.make_async_remote_copy(
                         src_ref=src,
                         dst_ref=back.at[head],
-                        send_sem=send2.at[c * targets + i],
-                        recv_sem=recv2.at[head],
+                        send_sem=send2,
+                        recv_sem=recv2.at[head // members],
                         device_id={"blk": d // ulys, "uly": d % ulys},
                         device_id_type=MESH,
                     ),
@@ -193,43 +187,43 @@
                 weighted, total = lax.fori_loop(
                     0, copies, functools.partial(lambda q, j, c: step(q, j, c), query), carry
                 )
-            attn[c] = (weighted / total).astype(jnp.bfloat16)
+            attn[pl.ds(pl.multiple_of(c * chunk, chunk), chunk), :] = (weighted / total).astype(jnp.bfloat16)
             for home, local, remote in result_copies(c):
                 pl.when(home)(lambda local=local: local().start())
                 pl.when(jnp.logical_not(home))(remote.start)
 
-        for c in range(chunks):
-            for home, _, remote in result_copies(c):
-                pl.when(jnp.logical_not(home))(remote.wait_send)
-
     load_w.wait()
     give_w.wait_recv()
-    first = (me * heads) // n
-    for i in range(heads):
-        h = lax.rem(first + i * (1 - 2 * upper) + heads, heads)
-        pltpu.make_async_copy(attn.at[0, pl.ds(0, rows)], back.at[h], recv2.at[h]).wait()
+    first = (me * groups) // n
+    for i in range(groups):
+        g = lax.rem(first + i * (1 - 2 * upper) + groups, groups)
+        take(back.at[pl.ds(g * members, members)], recv2.at[g])
         term = jnp.dot(
-            back[h, :, 0:HD],
-            w_vmem[pl.ds(pl.multiple_of(h * HD, HD), HD), :],
+            jnp.concatenate([back[g * members + j, :, 0:HD] for j in range(members)], axis=1),
+            w_vmem[pl.ds(pl.multiple_of(g * members * HD, members * HD), members * HD), :],
             preferred_element_type=jnp.float32,
         )
         if i == 0:
             acc[...] = term
-        elif i < heads - 1:
+        elif i < groups - 1:
             acc[...] += term
         else:
             out_ref[...] = (acc[...] + term).astype(out_ref.dtype)
 
     give_w.wait_send()
-
-    def sent(o):
-        d, copy = send_of(o)
-
-        @pl.when(d != me)
-        def _():
-            copy.wait_send()
-
-    loop(owners, sent)
+    for i in range(copies - 1):
+        take(pack, send1)
+
+    @pl.when(is_owner)
+    def _():
+        take(pack.at[pl.ds(0, heads - 1)], send1)
+        at_home = (slot % copies) * block == (me * rows) // block * block
+        pl.when(at_home)(lambda: take(attn.at[pl.ds(0, block - rows)], send2))
+        pl.when(jnp.logical_not(at_home))(lambda: take(attn, send2))
+
+    @pl.when(jnp.logical_not(is_owner))
+    def _():
+        take(pack, send1)
 
 
 def on_device(blks, ulys, query, key, value, q_gain, k_gain, out_weight):
@@ -243,7 +237,6 @@
     depth, cols = out_weight.shape
     seq = n * rows
     block = seq // copies
-    chunks = CHUNKS
     dma = pltpu.SemaphoreType.DMA
     return pl.pallas_call(
         functools.partial(layer_kernel, blks, ulys, heads, copies),
@@ -256,16 +249,16 @@
             pltpu.VMEM((width, cols), jnp.bfloat16),
             pltpu.VMEM((heads, rows, 3 * LANES), jnp.bfloat16),
             pltpu.VMEM((seq, 3 * LANES), jnp.bfloat16),
-            pltpu.VMEM((chunks, block // chunks, LANES), jnp.bfloat16),
+            pltpu.VMEM((block, LANES), jnp.bfloat16),
             pltpu.VMEM((heads, rows, LANES), jnp.bfloat16),
             pltpu.VMEM((rows, cols), jnp.float32),
             dma((3,)),
-            dma((2,)),
-            dma,
-            dma((owners,)),
-            dma((n,)),
-            dma((block // rows,)),
-            dma((heads,)),
+            dma,
+            dma,
+            dma,
+            dma,
+            dma,
+            dma((GROUPS,)),
             dma,
             dma,
         ],

time: 17.2 us -> 16.4 us (0.953)
  Pallas kernels: 16.5 us -> 15.6 us
    pallas_call x1, Pallas kernels: 16.5 us -> 15.6 us  [on_device(): pl.pallas_call(functools.partial(layer_kernel, blks, ulys, heads, copies)...]
where the time goes in v3:
time: 16.4 us; the launch traced here: 16.3 us
  Pallas kernels  15.6 us (95%)
  local copies, waits for them, and re-layouts  0.64 us (4%)
    pallas_call x1, Pallas kernels, on_device(): pl.pallas_call(functools.partial(layer_kernel, blks, ulys, heads, copies)...  15.6 us
    unnamed x1, local copies, waits for them, and re-layouts  0.64 us

profile of v3, /device:TPU:0, one launch (start us, length us, event | category | flops | bytes accessed | tf_op | source)
XLA Modules:
  0.0 16.3 jit_solution(3717375737630317878)
XLA Ops:
  0.0 15.6 %shard_map.64 = bf16[16,2304]{1,0:T(8,128)(2,1)S(1)} custom-call(bf16[16,1152]{1,0:T(8,128)(2,1)} %q_hbm.1, bf16[16,1152]{1,0:T(8,128)(2,1)} %k_hbm.1, bf16[16,1152]{1,0:T(8,128)(2,1)} %v_hbm.1, f32[1,96]{1,0:T(1,128)} %bitcast.2, f32[1,96]{1,0:T(1,128)} %bitcast.3, bf16[576,2304]{1,0:T(8,128)(2,1)} %w_hbm.1), custom_call_target="tpu_custom_call" | custom-call | tf_op jit(solution)/shard_map/pallas_call | solution.py:241
  15.6 0.6 %copy.8 = bf16[16,2304]{1,0:T(8,128)(2,1)} copy(bf16[16,2304]{1,0:T(8,128)(2,1)S(1)} %shard_map.64) | data formatting | bytes 147456

commit v4 on v3

--- a/solution.py
+++ b/solution.py
@@ -158,7 +158,8 @@
             return weighted, total
 
         def result_copies(c):
-            for i in range(targets):
+            for k in range(targets):
+                i = targets - 1 - k + upper * (2 * k + 1 - targets)
                 d = (part * chunks + c) * targets + i
                 src = attn.at[pl.ds(pl.multiple_of((c * targets + i) * rows, rows), rows)]
                 yield (
@@ -198,17 +199,19 @@
     for i in range(groups):
         g = lax.rem(first + i * (1 - 2 * upper) + groups, groups)
         take(back.at[pl.ds(g * members, members)], recv2.at[g])
-        term = jnp.dot(
-            jnp.concatenate([back[g * members + j, :, 0:HD] for j in range(members)], axis=1),
-            w_vmem[pl.ds(pl.multiple_of(g * members * HD, members * HD), members * HD), :],
-            preferred_element_type=jnp.float32,
-        )
-        if i == 0:
-            acc[...] = term
-        elif i < groups - 1:
-            acc[...] += term
-        else:
-            out_ref[...] = (acc[...] + term).astype(out_ref.dtype)
+        for j in range(members):
+            h = g * members + j
+            term = jnp.dot(
+                back[h, :, 0:HD],
+                w_vmem[pl.ds(pl.multiple_of(h * HD, HD), HD), :],
+                preferred_element_type=jnp.float32,
+            )
+            if i == 0 and j == 0:
+                acc[...] = term
+            elif i < groups - 1 or j < members - 1:
+                acc[...] += term
+            else:
+                out_ref[...] = (acc[...] + term).astype(out_ref.dtype)
 
     give_w.wait_send()
     for i in range(copies - 1):

time: 16.4 us -> 16.3 us (level)
  no operation moved by 1% of the time
where the time goes in v4:
time: 16.3 us; the launch traced here: 16.1 us
  Pallas kernels  15.5 us (95%)
  local copies, waits for them, and re-layouts  0.64 us (4%)
    pallas_call x1, Pallas kernels, on_device(): pl.pallas_call(functools.partial(layer_kernel, blks, ulys, heads, copies)...  15.5 us
    unnamed x1, local copies, waits for them, and re-layouts  0.64 us

profile of v4, /device:TPU:0, one launch (start us, length us, event | category | flops | bytes accessed | tf_op | source)
XLA Modules:
  0.0 16.1 jit_solution(2110501981419019633)
XLA Ops:
  0.0 15.5 %shard_map.64 = bf16[16,2304]{1,0:T(8,128)(2,1)S(1)} custom-call(bf16[16,1152]{1,0:T(8,128)(2,1)} %q_hbm.1, bf16[16,1152]{1,0:T(8,128)(2,1)} %k_hbm.1, bf16[16,1152]{1,0:T(8,128)(2,1)} %v_hbm.1, f32[1,96]{1,0:T(1,128)} %bitcast.2, f32[1,96]{1,0:T(1,128)} %bitcast.3, bf16[576,2304]{1,0:T(8,128)(2,1)} %w_hbm.1), custom_call_target="tpu_custom_call" | custom-call | tf_op jit(solution)/shard_map/pallas_call | solution.py:244
  15.5 0.6 %copy.8 = bf16[16,2304]{1,0:T(8,128)(2,1)} copy(bf16[16,2304]{1,0:T(8,128)(2,1)S(1)} %shard_map.64) | data formatting | bytes 147456
